TPU v7x, 32 devices: a whole 2x2x4 slice. The times are simulated.
32 devices in a mesh: ka: 8 (over y, x, core), ga: 4 (over z).
Axes of the slice: x: 2, y: 2, z: 4, core: 2. Of those that a mesh axis runs over, the one named last changes fastest.
Arguments:
- pair_densities: float32 [8192, 8192], P('ka', 'ga'), may hold values from -0.0625 to 0.0625
- energies: float32 [8192], P('ka'), may hold values from -2 to 2
- coulomb: float32 [8192], P('ga'), may hold values from 0.2 to 2
- start: float32 [8192, 128], P('ka'), may hold values from -6 to 6
Outputs:
- alphas: float32 [4, 128], replicated
- betas: float32 [4, 128], replicated
- lanczos_vector: float32 [8192, 128], P('ka')
All inputs are finite; a program needn't handle non-finite values.
Results may differ from a plain program's by a relative error of at most 0.00013.
Values sent between devices are 32-bit elements; how exact they have to be, the bound alone decides.
No kernel may reach another device: no remote copies, remote signals or barrier semaphores. Data moves between devices by JAX's collectives and lax.ppermute only.
A program may use at most 64 MiB of HBM per device.

v0:
```python
import jax
import jax.numpy as jnp
from jax import lax
from jax.sharding import PartitionSpec as P

ITERS = 4
EPSILON = 1e-06


def per_device(pair_densities, energies, coulomb, start):
    precise = lax.Precision.HIGHEST
    vector_count = start.shape[1]

    def project(full_vector, extra_rows):
        projected = jnp.dot(
            pair_densities.T, full_vector, precision=precise, preferred_element_type=jnp.float32
        )
        projected = jnp.concatenate([projected] + extra_rows, axis=0)
        return lax.psum(projected, "ka")

    start_sq = lax.psum(jnp.sum(start * start, axis=0), "ka")
    full_vector = start / jnp.sqrt(start_sq + EPSILON)
    vector = full_vector
    previous = jnp.zeros_like(vector)
    beta_now = jnp.zeros((vector_count,), jnp.float32)
    alpha_rows = []
    beta_rows = []
    remainder_full = full_vector
    remainder_own = vector
    for step in range(ITERS):
        energy_row = jnp.sum(energies[:, None] * remainder_full * remainder_full, axis=0)[None, :]
        if step == 0:
            summed = project(remainder_full, [energy_row])
            projected = summed[:-1]
            energy_sum = summed[-1]
            vector = remainder_own
        else:
            square_row = jnp.sum(remainder_full * remainder_full, axis=0)[None, :]
            summed = project(remainder_full, [square_row, energy_row])
            beta_full = jnp.sqrt(summed[-2] + EPSILON)
            projected = summed[:-2] / beta_full
            energy_sum = summed[-1] / (beta_full * beta_full)
            beta_new = beta_full
            beta_rows.append(beta_new)
            previous = vector
            vector = remainder_own / beta_new
            beta_now = beta_new
        weighted = coulomb[:, None] * projected
        curvature = jnp.sum(projected * weighted, axis=0)[None, :]
        partial_value = jnp.dot(
            pair_densities, weighted, precision=precise, preferred_element_type=jnp.float32
        )
        combine_partial_value = jnp.concatenate([partial_value, curvature], axis=0)
        combined = lax.psum(combine_partial_value, "ga")
        mixed = combined[:-1]
        alpha_now = energy_sum + combined[-1]
        image = energies[:, None] * vector + mixed
        remainder_own = image - alpha_now * vector - beta_now * previous
        alpha_rows.append(alpha_now)
        if step + 1 < ITERS:
            remainder_full = remainder_own
    last_sq = lax.psum(jnp.sum(remainder_own * remainder_own, axis=0), "ka")
    beta_new = jnp.sqrt(last_sq + EPSILON)
    beta_rows.append(beta_new)
    vector = remainder_own / beta_new
    alpha_table = jnp.stack(alpha_rows)
    beta_table = jnp.stack(beta_rows)
    full_vector = vector
    return (alpha_table, beta_table, full_vector)


def solution(mesh):
    placed = (P("ka", "ga"), P("ka"), P("ga"), P("ka", None))
    return jax.shard_map(
        per_device, mesh=mesh, in_specs=placed, out_specs=(P(), P(), P("ka", None)), check_vma=False
    )
```

profile of v0, /device:TPU:0, one launch (start us, length us, event | category | flops | bytes accessed | tf_op | source)
XLA Modules:
  0.0 530.7 jit_solution(17635808133581083179)
XLA Ops:
  7.2 1.2 multiply_reduce_fusion.4
  8.4 1.2 copy.39
  9.7 15.2 %psum.70 = f32[128]{0:T(128)S(1)} all-reduce(f32[128]{0:T(128)S(1)} %multiply_reduce_fusion.4), channel_id=1, replica_groups=mesh['ka'=8,'ga'=4] {'ka'}, use_global_device_ids=true, to_apply=%region_1.0 | all-reduce | flops 128 | bytes 1024 | tf_op jit(solution)/shard_map/psum | solution.py:21
  24.8 0.2 fusion.25
  25.2 7.1 %convolution_bitcast_fusion.3 = f32[2048,128]{0,1:T(8,128)S(1)} fusion(f32[1024,2048]{1,0:T(8,128)} %param.4, f32[1024,128]{0,1:T(8,128)S(1)} %copy.39, f32[128]{0:T(128)S(1)} %add_sqrt_fusion.1), kind=kOutput, calls=%fused_computation.3 | convolution fusion | flops 3221356544 | bytes 9961984 | tf_op jit(solution)/shard_map/dot_general | solution.py:15
  32.2 1.1 pad_maximum_fusion
  33.4 56.5 %all-reduce.9.cloned.1.call-done = f32[2049,128]{0,1:T(8,128)} async-done(((f32[2049,128]{0,1:T(8,128)}), f32[2049,128]{0,1:T(8,128)}) %all-reduce.9.cloned.1.call-update) | async-done | bytes 1049104 | tf_op jit(solution)/shard_map/psum | solution.py:19
  89.9 1.5 fusion.20
  91.5 11.1 %fusion.8 = f32[1024,128]{0,1:T(8,128)S(1)} fusion(f32[1024,2048]{1,0:T(8,128)} %param.4, f32[2049,128]{0,1:T(8,128)S(1)} %copy-done.3, f32[2048]{0:T(1024)S(1)} %copy-done.4), kind=kOutput, calls=%fused_computation.16 | convolution fusion | flops 3221487616 | bytes 9969664 | tf_op jit(solution)/shard_map/dot_general | solution.py:50
  102.6 0.9 pad_maximum_fusion.1
  103.6 39.1 %all-reduce.11.cloned.1.call-done = f32[1025,128]{0,1:T(8,128)} async-done(((f32[1025,128]{0,1:T(8,128)}), f32[1025,128]{0,1:T(8,128)}) %all-reduce.11.cloned.1.call-update) | async-done | bytes 524816 | tf_op jit(solution)/shard_map/psum | solution.py:54
  142.6 0.9 fusion.54
  143.6 1.4 fusion.27
  145.2 7.0 %convolution_bitcast_fusion.2 = f32[2048,128]{0,1:T(8,128)S(1)} fusion(f32[1024,128]{0,1:T(8,128)S(1)} %get-tuple-element.28, f32[1024,2048]{1,0:T(8,128)} %param.4), kind=kOutput, calls=%fused_computation.2 | convolution fusion | flops 3221225472 | bytes 9961472 | tf_op jit(solution)/shard_map/dot_general | solution.py:15
  152.2 1.2 concatenate.26
  153.7 56.4 %all-reduce.13.cloned.1.call-done = f32[2050,128]{0,1:T(8,128)} async-done(((f32[2050,128]{0,1:T(8,128)}), f32[2050,128]{0,1:T(8,128)}) %all-reduce.13.cloned.1.call-update) | async-done | bytes 1049616 | tf_op jit(solution)/shard_map/psum | solution.py:19
  210.1 1.0 fusion.42
  211.2 1.5 fusion.21
  212.8 10.9 %fusion.11 = f32[1024,128]{0,1:T(8,128)S(1)} fusion(f32[1024,2048]{1,0:T(8,128)} %param.4, f32[2048]{0:T(1024)S(1)} %copy-done.4, f32[2050,128]{0,1:T(8,128)S(1)} %copy-done.1, f32[128]{0:T(128)S(1)} %get-tuple-element.32), kind=kOutput, calls=%fused_computation.17 | convolution fusion | flops 3221749760 | bytes 9970176 | tf_op jit(solution)/shard_map/dot_general | solution.py:50
  223.7 0.9 pad_maximum_fusion.2
  224.6 39.0 %all-reduce.15.cloned.1.call-done = f32[1025,128]{0,1:T(8,128)} async-done(((f32[1025,128]{0,1:T(8,128)}), f32[1025,128]{0,1:T(8,128)}) %all-reduce.15.cloned.1.call-update) | async-done | bytes 524816 | tf_op jit(solution)/shard_map/psum | solution.py:54
  263.7 1.0 fusion.52
  264.7 1.4 fusion.28
  266.4 7.0 %convolution_bitcast_fusion.1 = f32[2048,128]{0,1:T(8,128)S(1)} fusion(f32[1024,128]{0,1:T(8,128)S(1)} %get-tuple-element.25, f32[1024,2048]{1,0:T(8,128)} %param.4), kind=kOutput, calls=%fused_computation.1 | convolution fusion | flops 3221225472 | bytes 9961472 | tf_op jit(solution)/shard_map/dot_general | solution.py:15
  273.4 1.2 concatenate.28
  274.7 56.6 %all-reduce.17.cloned.1.call-done = f32[2050,128]{0,1:T(8,128)} async-done(((f32[2050,128]{0,1:T(8,128)}), f32[2050,128]{0,1:T(8,128)}) %all-reduce.17.cloned.1.call-update) | async-done | bytes 1049616 | tf_op jit(solution)/shard_map/psum | solution.py:19
  331.3 1.0 fusion.41
  332.4 1.5 fusion.22
  334.0 10.9 %fusion.14 = f32[1024,128]{0,1:T(8,128)S(1)} fusion(f32[1024,2048]{1,0:T(8,128)} %param.4, f32[2048]{0:T(1024)S(1)} %copy-done.4, f32[2050,128]{0,1:T(8,128)S(1)} %copy-done.2, f32[128]{0:T(128)S(1)} %get-tuple-element.34), kind=kOutput, calls=%fused_computation.18 | convolution fusion | flops 3221749760 | bytes 9970176 | tf_op jit(solution)/shard_map/dot_general | solution.py:50
  344.9 0.9 pad_maximum_fusion.3
  345.8 0.3 all-reduce.21.cloned.1.call-start
  346.1 38.8 %all-reduce.19.cloned.1.call-done = f32[1025,128]{0,1:T(8,128)} async-done(((f32[1025,128]{0,1:T(8,128)}), f32[1025,128]{0,1:T(8,128)}) %all-reduce.19.cloned.1.call-update) | async-done | bytes 524816 | tf_op jit(solution)/shard_map/psum | solution.py:54
  384.9 1.0 fusion.50
  385.9 1.4 fusion.29
  387.6 7.0 %convolution_bitcast_fusion = f32[2048,128]{0,1:T(8,128)S(1)} fusion(f32[1024,128]{0,1:T(8,128)S(1)} %get-tuple-element.22, f32[1024,2048]{1,0:T(8,128)} %param.4), kind=kOutput, calls=%fused_computation | convolution fusion | flops 3221225472 | bytes 9961472 | tf_op jit(solution)/shard_map/dot_general | solution.py:15
  394.6 1.2 concatenate.30
  395.9 56.6 %all-reduce.21.cloned.1.call-done = f32[2050,128]{0,1:T(8,128)} async-done(((f32[2050,128]{0,1:T(8,128)}), f32[2050,128]{0,1:T(8,128)}) %all-reduce.21.cloned.1.call-update) | async-done | bytes 1049616 | tf_op jit(solution)/shard_map/psum | solution.py:19
  452.5 1.0 fusion.40
  453.6 1.5 fusion.23
  455.2 10.9 %fusion.17 = f32[1024,128]{0,1:T(8,128)S(1)} fusion(f32[1024,2048]{1,0:T(8,128)} %param.4, f32[2048]{0:T(1024)S(1)} %copy-done.4, f32[2050,128]{0,1:T(8,128)S(1)} %copy-done, f32[128]{0:T(128)S(1)} %get-tuple-element.36), kind=kOutput, calls=%fused_computation.19 | convolution fusion | flops 3221749760 | bytes 9970176 | tf_op jit(solution)/shard_map/dot_general | solution.py:50
  466.1 0.9 pad_maximum_fusion.4
  467.5 38.6 %all-reduce.23.cloned.1.call-done = f32[1025,128]{0,1:T(8,128)} async-done(((f32[1025,128]{0,1:T(8,128)}), f32[1025,128]{0,1:T(8,128)}) %all-reduce.23.cloned.1.call-update) | async-done | bytes 524816 | tf_op jit(solution)/shard_map/psum | solution.py:54
  506.1 1.0 fusion.48
  507.1 1.4 multiply_reduce_fusion
  508.5 13.0 %psum.79 = f32[128]{0:T(128)S(1)} all-reduce(f32[128]{0:T(128)S(1)} %get-tuple-element.18), channel_id=1, replica_groups=mesh['ka'=8,'ga'=4] {'ka'}, use_global_device_ids=true, to_apply=%region_22.0 | all-reduce | flops 128 | bytes 1024 | tf_op jit(solution)/shard_map/psum | solution.py:62
  521.7 1.0 copy.58
  522.7 0.6 pad_maximum_fusion.5
  523.3 0.6 pad_maximum_fusion.6
  (48 shorter events, 2.5 us)
Async XLA Ops:
  7.2 17.7 %copy-start.5 = (f32[1024]{0:T(1024)S(1)}, f32[1024]{0:T(1024)}, u32[]{:S(2)}) copy-start(f32[1024]{0:T(1024)} %param.5) | copy-start | bytes 12292
  7.2 82.7 %all-reduce.9.cloned.1.call-start = ((), (), s32[]{:S(2)}) async-start(), calls=%async_computation | async-start | bytes 2228224 | tf_op jit(solution)/shard_map/psum | solution.py:19
  33.4 56.6 %copy-start.4 = (f32[2048]{0:T(1024)S(1)}, f32[2048]{0:T(1024)}, u32[]{:S(2)}) copy-start(f32[2048]{0:T(1024)} %param.6) | copy-start | bytes 24580
  33.4 109.2 %all-reduce.11.cloned.1.call-start = ((), (), s32[]{:S(2)}) async-start(), calls=%async_computation.1 | async-start | bytes 1179648 | tf_op jit(solution)/shard_map/psum | solution.py:54
  89.9 1.6 copy-start.3
  103.5 106.6 %all-reduce.13.cloned.1.call-start = ((), (), s32[]{:S(2)}) async-start(), calls=%async_computation.2 | async-start | bytes 2228224 | tf_op jit(solution)/shard_map/psum | solution.py:19
  153.5 110.2 %all-reduce.15.cloned.1.call-start = ((), (), s32[]{:S(2)}) async-start(), calls=%async_computation.3 | async-start | bytes 1179648 | tf_op jit(solution)/shard_map/psum | solution.py:54
  210.1 2.7 copy-start.1
  224.6 106.7 %all-reduce.17.cloned.1.call-start = ((), (), s32[]{:S(2)}) async-start(), calls=%async_computation.4 | async-start | bytes 2228224 | tf_op jit(solution)/shard_map/psum | solution.py:19
  274.7 110.2 %all-reduce.19.cloned.1.call-start = ((), (), s32[]{:S(2)}) async-start(), calls=%async_computation.5 | async-start | bytes 1179648 | tf_op jit(solution)/shard_map/psum | solution.py:54
  331.3 2.7 copy-start.2
  345.8 106.7 %all-reduce.21.cloned.1.call-start = ((), (), s32[]{:S(2)}) async-start(), calls=%async_computation.6 | async-start | bytes 2228224 | tf_op jit(solution)/shard_map/psum | solution.py:19
  395.8 110.2 %all-reduce.23.cloned.1.call-start = ((), (), s32[]{:S(2)}) async-start(), calls=%async_computation.7 | async-start | bytes 1179648 | tf_op jit(solution)/shard_map/psum | solution.py:54
  452.5 2.7 copy-start
Sparse Core Ops, SparseCore 0:
  33.5 56.3 all-reduce.8
  103.7 38.9 all-reduce.10
  153.6 56.4 all-reduce.12
  224.7 38.9 all-reduce.14
  274.8 56.4 all-reduce.16
  345.9 38.9 all-reduce.18
  396.0 56.4 all-reduce.20
  467.1 38.9 all-reduce.22
where the time goes:
time: 531 us
  waiting for transfers between devices  382 us (72%)
  matrix products  71.9 us (14%)
  blocking collectives  28.1 us (5%)
  other arithmetic  26.1 us (5%)
  between operations  14.3 us (3%)
  local copies, waits for them, and re-layouts  7.71 us (1%)
    psum x4, waiting for transfers between devices, project(): return lax.psum(projected, 'ka')  226 us
    psum x4, waiting for transfers between devices, per_device(): combined = lax.psum(combine_partial_value, 'ga')  156 us
    dot_general x4, matrix products, per_device(): jnp.dot(pair_densities, weighted, precision=precise, preferred_element_ty...  43.8 us
    dot_general x4, matrix products, project(): jnp.dot(pair_densities.T, full_vector, precision=precise, preferred_eleme...  28.1 us
    psum x1, blocking collectives, per_device(): start_sq = lax.psum(jnp.sum(start * start, axis=0), 'ka')  15.2 us
    psum x1, blocking collectives, per_device(): last_sq = lax.psum(jnp.sum(remainder_own * remainder_own, axis=0), 'ka')  13 us
  transfers between devices with their start and end apart: 8, of which 8 were waited for; matrix products, arithmetic and copies ran while one was open for 0% of the time, Pallas kernels for 0%

commit v1 on v0

--- a/solution.py
+++ b/solution.py
@@ -5,6 +5,15 @@
 
 ITERS = 4
 EPSILON = 1e-06
+
+
+def add_in_pairs(x, axis):
+    count = lax.axis_size(axis)
+    total, far = (x, 1)
+    while far < count:
+        total = total + lax.ppermute(total, axis, [(i, i ^ far) for i in range(count)])
+        far = 2 * far
+    return total
 
 
 def per_device(pair_densities, energies, coulomb, start):
@@ -51,7 +60,7 @@
             pair_densities, weighted, precision=precise, preferred_element_type=jnp.float32
         )
         combine_partial_value = jnp.concatenate([partial_value, curvature], axis=0)
-        combined = lax.psum(combine_partial_value, "ga")
+        combined = add_in_pairs(combine_partial_value, "ga")
         mixed = combined[:-1]
         alpha_now = energy_sum + combined[-1]
         image = energies[:, None] * vector + mixed

time: 531 us -> 557 us (1.049); the launches traced: 531 us -> 549 us
  matrix products: 71.9 us -> 107 us
  waiting for transfers between devices: 382 us -> 361 us
  starting transfers between devices: 0.73 us -> 16 us
  other arithmetic: 26.1 us -> 17.2 us
    psum x4 -> x0, waiting for transfers between devices: 156 us -> none  [per_device(): combined = lax.psum(combine_partial_value, 'ga')]
    ppermute x0 -> x8, waiting for transfers between devices: none -> 134 us  [add_in_pairs(): lax.ppermute(total, axis, [(i, i ^ far) for i in range(count)])]
    dot_general x4, matrix products: 28.1 us -> 68.2 us  [project(): jnp.dot(pair_densities.T, full_vector, precision=precise, preferred_eleme...]
    ppermute x0 -> x8, starting transfers between devices: none -> 15.8 us  [add_in_pairs(): lax.ppermute(total, axis, [(i, i ^ far) for i in range(count)])]
  transfers between devices with their start and end apart: 8 -> 12, of which waited for: 8 -> 12; matrix products, arithmetic and copies ran while one was open for 0% -> 0% of each run, Pallas kernels for 0% -> 0%
where the time goes in v1:
time: 557 us; the launch traced here: 549 us
  waiting for transfers between devices  361 us (65%)
  matrix products  107 us (19%)
  blocking collectives  26.9 us (5%)
  other arithmetic  17.2 us (3%)
  starting transfers between devices  16 us (3%)
  between operations  14.2 us (3%)
  local copies, waits for them, and re-layouts  6.74 us (1%)
    psum x4, waiting for transfers between devices, project(): return lax.psum(projected, 'ka')  226 us
    ppermute x8, waiting for transfers between devices, add_in_pairs(): lax.ppermute(total, axis, [(i, i ^ far) for i in range(count)])  134 us
    dot_general x4, matrix products, project(): jnp.dot(pair_densities.T, full_vector, precision=precise, preferred_eleme...  68.2 us
    dot_general x4, matrix products, per_device(): jnp.dot(pair_densities, weighted, precision=precise, preferred_element_ty...  39.2 us
    ppermute x8, starting transfers between devices, add_in_pairs(): lax.ppermute(total, axis, [(i, i ^ far) for i in range(count)])  15.8 us
    psum x1, blocking collectives, per_device(): start_sq = lax.psum(jnp.sum(start * start, axis=0), 'ka')  15.1 us
    psum x1, blocking collectives, per_device(): last_sq = lax.psum(jnp.sum(remainder_own * remainder_own, axis=0), 'ka')  11.8 us
  transfers between devices with their start and end apart: 12, of which 12 were waited for; matrix products, arithmetic and copies ran while one was open for 0% of the time, Pallas kernels for 0%

profile of v1, /device:TPU:0, one launch (start us, length us, event | category | flops | bytes accessed | tf_op | source)
XLA Modules:
  0.0 549.2 jit_solution(14285285475619719911)
XLA Ops:
  7.2 1.2 multiply_reduce_fusion.4
  8.5 15.1 %psum.42 = f32[128]{0:T(128)S(1)} all-reduce(f32[128]{0:T(128)S(1)} %multiply_reduce_fusion.4), channel_id=1, replica_groups=mesh['ka'=8,'ga'=4] {'ka'}, use_global_device_ids=true, to_apply=%region_1.0 | all-reduce | flops 128 | bytes 1024 | tf_op jit(solution)/shard_map/psum | solution.py:30
  23.6 1.3 fusion.25
  24.9 15.6 %convolution_bitcast_fusion.3 = f32[2048,128]{1,0:T(8,128)S(1)} fusion(f32[1024,2048]{1,0:T(8,128)} %param.4, f32[1024,128]{1,0:T(8,128)S(1)} %copy-done, f32[128]{0:T(128)S(1)} %add_sqrt_fusion.1), kind=kOutput, calls=%fused_computation.3 | convolution fusion | flops 3221356544 | bytes 9961984 | tf_op jit(solution)/shard_map/dot_general | solution.py:24
  40.5 1.1 pad_maximum_fusion
  41.6 56.3 %all-reduce.5.cloned.1.call-done = f32[2049,128]{1,0:T(8,128)} async-done(((f32[2049,128]{1,0:T(8,128)}), f32[2049,128]{1,0:T(8,128)}) %all-reduce.5.cloned.1.call-update) | async-done | bytes 1049104 | tf_op jit(solution)/shard_map/psum | solution.py:28
  98.0 1.7 fusion.20
  99.7 9.9 %fusion.8 = f32[1024,128]{1,0:T(8,128)S(1)} fusion(f32[1024,2048]{1,0:T(8,128)} %param.4, f32[2049,128]{1,0:T(8,128)} %all-reduce.5.cloned.1.call-done, f32[2048]{0:T(1024)S(1)} %copy-done.4), kind=kOutput, calls=%fused_computation.16 | convolution fusion | flops 3221487616 | bytes 9969664 | tf_op jit(solution)/shard_map/dot_general | solution.py:59
  109.7 1.5 collective-permute-start
  111.1 11.6 %collective-permute-done = f32[1025,128]{1,0:T(8,128)S(1)} collective-permute-done((f32[1025,128]{1,0:T(8,128)S(1)}, f32[1025,128]{1,0:T(8,128)S(1)}, u32[]{:S(2)}, u32[]{:S(2)}) %collective-permute-start) | collective-permute-done | bytes 524832 | tf_op jit(solution)/shard_map/ppermute | solution.py:14
  122.8 2.5 collective-permute-start.1
  125.3 22.0 %collective-permute-done.1 = f32[1025,128]{1,0:T(8,128)S(1)} collective-permute-done((f32[1025,128]{1,0:T(8,128)S(1)}, f32[1025,128]{1,0:T(8,128)S(1)}, u32[]{:S(2)}, u32[]{:S(2)}) %collective-permute-start.1) | collective-permute-done | bytes 524832 | tf_op jit(solution)/shard_map/ppermute | solution.py:14
  147.4 0.7 slice_add_fusion.9
  148.3 25.7 %convolution_bitcast_fusion.2 = f32[2048,128]{1,0:T(8,128)S(1)} fusion(f32[1024,128]{1,0:T(8,128)S(1)} %get-tuple-element.22, f32[1024,2048]{1,0:T(8,128)S(1)} %bitcast.51), kind=kOutput, calls=%fused_computation.2 | convolution fusion | flops 3221225472 | bytes 9961472 | tf_op jit(solution)/shard_map/dot_general | solution.py:24
  174.0 2.2 concatenate.26
  176.3 56.6 %all-reduce.7.cloned.1.call-done = f32[2050,128]{1,0:T(8,128)} async-done(((f32[2050,128]{1,0:T(8,128)}), f32[2050,128]{1,0:T(8,128)}) %all-reduce.7.cloned.1.call-update) | async-done | bytes 1049616 | tf_op jit(solution)/shard_map/psum | solution.py:28
  232.9 0.8 fusion.42
  233.7 1.7 fusion.21
  235.4 10.1 %fusion.11 = f32[1024,128]{1,0:T(8,128)S(1)} fusion(f32[1024,2048]{1,0:T(8,128)} %param.4, f32[2048]{0:T(1024)S(1)} %copy-done.4, f32[2050,128]{1,0:T(8,128)S(1)} %copy-done.1, f32[128]{0:T(128)S(1)} %get-tuple-element.24), kind=kOutput, calls=%fused_computation.17 | convolution fusion | flops 3221749760 | bytes 9970176 | tf_op jit(solution)/shard_map/dot_general | solution.py:59
  245.6 1.5 collective-permute-start.2
  247.0 11.6 %collective-permute-done.2 = f32[1025,128]{1,0:T(8,128)S(1)} collective-permute-done((f32[1025,128]{1,0:T(8,128)S(1)}, f32[1025,128]{1,0:T(8,128)S(1)}, u32[]{:S(2)}, u32[]{:S(2)}) %collective-permute-start.2) | collective-permute-done | bytes 524832 | tf_op jit(solution)/shard_map/ppermute | solution.py:14
  258.7 2.5 collective-permute-start.3
  261.2 22.0 %collective-permute-done.3 = f32[1025,128]{1,0:T(8,128)S(1)} collective-permute-done((f32[1025,128]{1,0:T(8,128)S(1)}, f32[1025,128]{1,0:T(8,128)S(1)}, u32[]{:S(2)}, u32[]{:S(2)}) %collective-permute-start.3) | collective-permute-done | bytes 524832 | tf_op jit(solution)/shard_map/ppermute | solution.py:14
  283.3 0.3 fusion.28
  283.6 13.6 %convolution_bitcast_fusion.1 = f32[2048,128]{1,0:T(8,128)S(1)} fusion(f32[1024,128]{1,0:T(8,128)S(1)} %get-tuple-element.21, f32[1024,2048]{1,0:T(8,128)S(1)} %bitcast.53), kind=kOutput, calls=%fused_computation.1 | convolution fusion | flops 3221225472 | bytes 9961472 | tf_op jit(solution)/shard_map/dot_general | solution.py:24
  297.2 2.2 concatenate.28
  299.5 56.6 %all-reduce.9.cloned.1.call-done = f32[2050,128]{1,0:T(8,128)} async-done(((f32[2050,128]{1,0:T(8,128)}), f32[2050,128]{1,0:T(8,128)}) %all-reduce.9.cloned.1.call-update) | async-done | bytes 1049616 | tf_op jit(solution)/shard_map/psum | solution.py:28
  356.1 0.8 fusion.41
  356.9 1.7 fusion.22
  358.6 10.1 %fusion.14 = f32[1024,128]{1,0:T(8,128)S(1)} fusion(f32[1024,2048]{1,0:T(8,128)} %param.4, f32[2048]{0:T(1024)S(1)} %copy-done.4, f32[2050,128]{1,0:T(8,128)S(1)} %copy-done.2, f32[128]{0:T(128)S(1)} %get-tuple-element.26), kind=kOutput, calls=%fused_computation.18 | convolution fusion | flops 3221749760 | bytes 9970176 | tf_op jit(solution)/shard_map/dot_general | solution.py:59
  368.7 1.5 collective-permute-start.4
  370.2 11.6 %collective-permute-done.4 = f32[1025,128]{1,0:T(8,128)S(1)} collective-permute-done((f32[1025,128]{1,0:T(8,128)S(1)}, f32[1025,128]{1,0:T(8,128)S(1)}, u32[]{:S(2)}, u32[]{:S(2)}) %collective-permute-start.4) | collective-permute-done | bytes 524832 | tf_op jit(solution)/shard_map/ppermute | solution.py:14
  381.9 2.5 collective-permute-start.5
  384.4 22.0 %collective-permute-done.5 = f32[1025,128]{1,0:T(8,128)S(1)} collective-permute-done((f32[1025,128]{1,0:T(8,128)S(1)}, f32[1025,128]{1,0:T(8,128)S(1)}, u32[]{:S(2)}, u32[]{:S(2)}) %collective-permute-start.5) | collective-permute-done | bytes 524832 | tf_op jit(solution)/shard_map/ppermute | solution.py:14
  406.8 13.3 %convolution_bitcast_fusion = f32[2048,128]{1,0:T(8,128)S(1)} fusion(f32[1024,128]{1,0:T(8,128)S(1)} %get-tuple-element.20, f32[1024,2048]{1,0:T(8,128)S(1)} %bitcast.55), kind=kOutput, calls=%fused_computation | convolution fusion | flops 3221225472 | bytes 9961472 | tf_op jit(solution)/shard_map/dot_general | solution.py:24
  420.1 2.2 concatenate.30
  422.4 56.7 %all-reduce.11.cloned.1.call-done = f32[2050,128]{1,0:T(8,128)} async-done(((f32[2050,128]{1,0:T(8,128)}), f32[2050,128]{1,0:T(8,128)}) %all-reduce.11.cloned.1.call-update) | async-done | bytes 1049616 | tf_op jit(solution)/shard_map/psum | solution.py:28
  479.1 0.8 fusion.40
  479.8 1.6 fusion.23
  481.4 9.2 %fusion.17 = f32[1024,128]{1,0:T(8,128)S(1)} fusion(f32[1024,2048]{1,0:T(8,128)} %param.4, f32[2048]{0:T(1024)S(1)} %copy-done.4, f32[2050,128]{1,0:T(8,128)S(1)} %copy-done.3, f32[128]{0:T(128)S(1)} %get-tuple-element.28), kind=kOutput, calls=%fused_computation.19 | convolution fusion | flops 3221749760 | bytes 9970176 | tf_op jit(solution)/shard_map/dot_general | solution.py:59
  490.7 1.5 collective-permute-start.6
  492.2 11.6 %collective-permute-done.6 = f32[1025,128]{1,0:T(8,128)S(1)} collective-permute-done((f32[1025,128]{1,0:T(8,128)S(1)}, f32[1025,128]{1,0:T(8,128)S(1)}, u32[]{:S(2)}, u32[]{:S(2)}) %collective-permute-start.6) | collective-permute-done | bytes 524832 | tf_op jit(solution)/shard_map/ppermute | solution.py:14
  503.9 2.5 collective-permute-start.7
  506.3 22.0 %collective-permute-done.7 = f32[1025,128]{1,0:T(8,128)S(1)} collective-permute-done((f32[1025,128]{1,0:T(8,128)S(1)}, f32[1025,128]{1,0:T(8,128)S(1)}, u32[]{:S(2)}, u32[]{:S(2)}) %collective-permute-start.7) | collective-permute-done | bytes 524832 | tf_op jit(solution)/shard_map/ppermute | solution.py:14
  528.4 0.6 pad_maximum_fusion.5
  529.3 11.8 %psum.47 = f32[128]{0:T(128)S(1)} all-reduce(f32[128]{0:T(128)S(1)} %get-tuple-element.18), channel_id=1, replica_groups=mesh['ka'=8,'ga'=4] {'ka'}, use_global_device_ids=true, to_apply=%region_18.0 | all-reduce | flops 128 | bytes 1024 | tf_op jit(solution)/shard_map/psum | solution.py:71
  541.1 0.8 broadcast_divide_fusion
  541.9 0.6 pad_maximum_fusion.6
  (55 shorter events, 1.8 us)
Async XLA Ops:
  7.2 17.7 %copy-start = (f32[1024,128]{1,0:T(8,128)S(1)}, f32[1024,128]{1,0:T(8,128)}, u32[]{:S(2)}) copy-start(f32[1024,128]{1,0:T(8,128)} %param.7) | copy-start | bytes 1572868
  7.2 90.8 %all-reduce.5.cloned.1.call-start = ((), (), s32[]{:S(2)}) async-start(), calls=%async_computation | async-start | bytes 2105344 | tf_op jit(solution)/shard_map/psum | solution.py:28
  41.6 56.4 %copy-start.4 = (f32[2048]{0:T(1024)S(1)}, f32[2048]{0:T(1024)}, u32[]{:S(2)}) copy-start(f32[2048]{0:T(1024)} %param.6) | copy-start | bytes 24580
  41.6 191.3 %all-reduce.7.cloned.1.call-start = ((), (), s32[]{:S(2)}) async-start(), calls=%async_computation.1 | async-start | bytes 2105344 | tf_op jit(solution)/shard_map/psum | solution.py:28
  98.0 50.3 %slice-start = ((s8[8388608]{0:T(1024)(128)(4,1)}), s8[4194304]{0:T(1024)(128)(4,1)S(1)}, s32[]{:S(2)}) async-start(s8[8388608]{0:T(1024)(128)(4,1)} %bitcast.50), calls=%async_computation.4 | async-start | bytes 8388608
  99.7 48.6 %slice-start.1 = ((s8[8388608]{0:T(1024)(128)(4,1)}), s8[4194304]{0:T(1024)(128)(4,1)S(1)}, s32[]{:S(2)}) async-start(s8[8388608]{0:T(1024)(128)(4,1)} %bitcast.50), calls=%async_computation.5 | async-start | bytes 8388608
  109.7 13.1 %collective-permute-start = (f32[1025,128]{1,0:T(8,128)S(1)}, f32[1025,128]{1,0:T(8,128)S(1)}, u32[]{:S(2)}, u32[]{:S(2)}) collective-permute-start(f32[1025,128]{1,0:T(8,128)S(1)} %pad_maximum_fusion.1), channel_id=1, source_target_pairs={{0,1},{1,0},{2,3},{3,2},{4,5},{5,4},{6,7},{7,6},{8,9},{9,8},{10,11... | collective-permute-start | bytes 1574408 | tf_op jit(solution)/shard_map/ppermute | solution.py:14
  122.8 25.2 %copy-start.5 = (f32[1024]{0:T(1024)S(1)}, f32[1024]{0:T(1024)}, u32[]{:S(2)}) copy-start(f32[1024]{0:T(1024)} %param.5) | copy-start | bytes 12292
  122.8 24.5 %collective-permute-start.1 = (f32[1025,128]{1,0:T(8,128)S(1)}, f32[1025,128]{1,0:T(8,128)S(1)}, u32[]{:S(2)}, u32[]{:S(2)}) collective-permute-start(f32[1025,128]{1,0:T(8,128)S(1)} %fusion.50), channel_id=1, source_target_pairs={{0,2},{1,3},{2,0},{3,1},{4,6},{5,7},{6,4},{7,5},{8,10},{9,11},{10,... | collective-permute-start | bytes 1574408 | tf_op jit(solution)/shard_map/ppermute | solution.py:14
  176.3 179.8 %all-reduce.9.cloned.1.call-start = ((), (), s32[]{:S(2)}) async-start(), calls=%async_computation.2 | async-start | bytes 2105344 | tf_op jit(solution)/shard_map/psum | solution.py:28
  232.9 2.5 copy-start.1
  233.7 49.9 %slice-start.2 = ((s8[8388608]{0:T(1024)(128)(4,1)}), s8[4194304]{0:T(1024)(128)(4,1)S(1)}, s32[]{:S(2)}) async-start(s8[8388608]{0:T(1024)(128)(4,1)} %bitcast.52), calls=%async_computation.6 | async-start | bytes 8388608
  235.4 48.2 %slice-start.3 = ((s8[8388608]{0:T(1024)(128)(4,1)}), s8[4194304]{0:T(1024)(128)(4,1)S(1)}, s32[]{:S(2)}) async-start(s8[8388608]{0:T(1024)(128)(4,1)} %bitcast.52), calls=%async_computation.7 | async-start | bytes 8388608
  245.6 13.1 %collective-permute-start.2 = (f32[1025,128]{1,0:T(8,128)S(1)}, f32[1025,128]{1,0:T(8,128)S(1)}, u32[]{:S(2)}, u32[]{:S(2)}) collective-permute-start(f32[1025,128]{1,0:T(8,128)S(1)} %pad_maximum_fusion.2), channel_id=1, source_target_pairs={{0,1},{1,0},{2,3},{3,2},{4,5},{5,4},{6,7},{7,6},{8,9},{9,8},{10,11... | collective-permute-start | bytes 1574408 | tf_op jit(solution)/shard_map/ppermute | solution.py:14
  258.7 24.5 %collective-permute-start.3 = (f32[1025,128]{1,0:T(8,128)S(1)}, f32[1025,128]{1,0:T(8,128)S(1)}, u32[]{:S(2)}, u32[]{:S(2)}) collective-permute-start(f32[1025,128]{1,0:T(8,128)S(1)} %fusion.49), channel_id=1, source_target_pairs={{0,2},{1,3},{2,0},{3,1},{4,6},{5,7},{6,4},{7,5},{8,10},{9,11},{10,... | collective-permute-start | bytes 1574408 | tf_op jit(solution)/shard_map/ppermute | solution.py:14
  299.5 179.6 %all-reduce.11.cloned.1.call-start = ((), (), s32[]{:S(2)}) async-start(), calls=%async_computation.3 | async-start | bytes 2105344 | tf_op jit(solution)/shard_map/psum | solution.py:28
  356.1 2.5 copy-start.2
  356.9 49.9 %slice-start.4 = ((s8[8388608]{0:T(1024)(128)(4,1)}), s8[4194304]{0:T(1024)(128)(4,1)S(1)}, s32[]{:S(2)}) async-start(s8[8388608]{0:T(1024)(128)(4,1)} %bitcast.54), calls=%async_computation.8 | async-start | bytes 8388608
  358.6 48.2 %slice-start.5 = ((s8[8388608]{0:T(1024)(128)(4,1)}), s8[4194304]{0:T(1024)(128)(4,1)S(1)}, s32[]{:S(2)}) async-start(s8[8388608]{0:T(1024)(128)(4,1)} %bitcast.54), calls=%async_computation.9 | async-start | bytes 8388608
  368.7 13.1 %collective-permute-start.4 = (f32[1025,128]{1,0:T(8,128)S(1)}, f32[1025,128]{1,0:T(8,128)S(1)}, u32[]{:S(2)}, u32[]{:S(2)}) collective-permute-start(f32[1025,128]{1,0:T(8,128)S(1)} %pad_maximum_fusion.3), channel_id=1, source_target_pairs={{0,1},{1,0},{2,3},{3,2},{4,5},{5,4},{6,7},{7,6},{8,9},{9,8},{10,11... | collective-permute-start | bytes 1574408 | tf_op jit(solution)/shard_map/ppermute | solution.py:14
  381.9 24.5 %collective-permute-start.5 = (f32[1025,128]{1,0:T(8,128)S(1)}, f32[1025,128]{1,0:T(8,128)S(1)}, u32[]{:S(2)}, u32[]{:S(2)}) collective-permute-start(f32[1025,128]{1,0:T(8,128)S(1)} %fusion.48), channel_id=1, source_target_pairs={{0,2},{1,3},{2,0},{3,1},{4,6},{5,7},{6,4},{7,5},{8,10},{9,11},{10,... | collective-permute-start | bytes 1574408 | tf_op jit(solution)/shard_map/ppermute | solution.py:14
  479.1 2.4 copy-start.3
  490.7 13.1 %collective-permute-start.6 = (f32[1025,128]{1,0:T(8,128)S(1)}, f32[1025,128]{1,0:T(8,128)S(1)}, u32[]{:S(2)}, u32[]{:S(2)}) collective-permute-start(f32[1025,128]{1,0:T(8,128)S(1)} %pad_maximum_fusion.4), channel_id=1, source_target_pairs={{0,1},{1,0},{2,3},{3,2},{4,5},{5,4},{6,7},{7,6},{8,9},{9,8},{10,11... | collective-permute-start | bytes 1574408 | tf_op jit(solution)/shard_map/ppermute | solution.py:14
  503.9 24.5 %collective-permute-start.7 = (f32[1025,128]{1,0:T(8,128)S(1)}, f32[1025,128]{1,0:T(8,128)S(1)}, u32[]{:S(2)}, u32[]{:S(2)}) collective-permute-start(f32[1025,128]{1,0:T(8,128)S(1)} %fusion.47), channel_id=1, source_target_pairs={{0,2},{1,3},{2,0},{3,1},{4,6},{5,7},{6,4},{7,5},{8,10},{9,11},{10,... | collective-permute-start | bytes 1574408 | tf_op jit(solution)/shard_map/ppermute | solution.py:14
Sparse Core Ops, SparseCore 0:
  41.7 56.2 all-reduce.4
  176.4 56.4 all-reduce.6
  299.6 56.4 all-reduce.8
  422.5 56.5 all-reduce.10
